TPU v7x, 32 devices: a whole 2x2x4 slice. The times are simulated.
32 devices in a mesh: seq: 8 (over z, x), head: 4 (over y, core).
Axes of the slice: x: 2, y: 2, z: 4, core: 2. Of those that a mesh axis runs over, the one named last changes fastest.
Arguments:
- xs: bfloat16 [8192, 4096], P('seq', 'head'), may hold values from -6 to 6
- gate_branch: bfloat16 [8192, 4096], P('seq', 'head'), may hold values from -6 to 6
- bmat: bfloat16 [8192, 128], P('seq'), may hold values from -0.375 to 0.375
- cmat: bfloat16 [8192, 128], P('seq'), may hold values from -0.375 to 0.375
- dt_code: int32 [64, 8192], P('head', 'seq'), may hold values from 1 to 32768
- resets: int32 [8192], P('seq'), may hold values 0 or 1
- decay_rate: float32 [64], P('head'), may hold values from 4.8828125e-05 to 0.08, as said below
- skip: float32 [64], P('head'), may hold values from 0.5 to 1.5
- norm_gain: float32 [4096], P('head'), may hold values from 0.1 to 1.9
- out_weight: bfloat16 [4096, 4096], P('head'), may hold values from -0.09375 to 0.09375
Outputs:
- mixed: bfloat16 [8192, 4096], P(('seq', 'head'))
Inputs may be any that keep to these rules, and one draw needn't show every extreme that they name: `decay_rate`: positive rates.
All inputs are finite; a program needn't handle non-finite values. No bound on the sum of `resets` on one device may be relied on, other than what follows from the above.
Results may differ from a plain program's by a relative error of at most 0.023.
Values may be sent and summed in bfloat16 or wider, within the bound.
A program may use at most 128 MiB of HBM per device.

v0:
```python
import jax
import jax.numpy as jnp
from jax import lax
from jax.sharding import PartitionSpec as P

HEAD_DIM = 64
STATE = 128
SPAN = 256
INNER = 4096


def local(xs, gate_branch, bmat, cmat, dt_code, resets, decay_rate, skip, norm_gain, out_weight):
    tokens_here = xs.shape[0]
    local_heads = dt_code.shape[0]
    blocks = tokens_here // SPAN
    step_size = dt_code.astype(jnp.float32) / 16.0
    input_scale = jnp.minimum(step_size, 1.0)
    logarithmic_damping = -decay_rate[:, None] * step_size
    cumulative = jnp.cumsum(logarithmic_damping.reshape(local_heads, blocks, SPAN), axis=2)
    counts = jnp.cumsum(resets.reshape(blocks, SPAN), axis=1)
    position = jnp.arange(SPAN)
    linked = (counts[:, :, None] == counts[:, None, :]) & (position[None, :] <= position[:, None])[
        None
    ]
    gaps = jnp.where(linked[None], cumulative[:, :, :, None] - cumulative[:, :, None, :], 0.0)
    within = jnp.where(linked[None], jnp.exp(gaps), 0.0)
    key_blocks = bmat.reshape(blocks, SPAN, STATE)
    query_blocks = cmat.reshape(blocks, SPAN, STATE)
    intersection = jnp.einsum(
        "cin,cjn->cij", query_blocks, key_blocks, preferred_element_type=jnp.float32
    )
    raw_values = xs.reshape(blocks, SPAN, local_heads, HEAD_DIM)
    step_scale = input_scale.reshape(local_heads, blocks, SPAN).transpose(1, 2, 0)[:, :, :, None]
    scaled = (raw_values.astype(jnp.float32) * step_scale).astype(jnp.bfloat16)
    scores = (within * intersection[None]).astype(jnp.bfloat16)
    intra = jnp.einsum("hcij,cjhp->cihp", scores, scaled, preferred_element_type=jnp.float32)
    to_end = jnp.where(
        counts[None] == counts[None, :, -1:], jnp.exp(cumulative[:, :, -1:] - cumulative), 0.0
    )
    through = jnp.where(counts[None, :, -1] == 0, jnp.exp(cumulative[:, :, -1]), 0.0)
    from_start = jnp.where(counts[None] == 0, jnp.exp(cumulative), 0.0)
    weighted = (scaled.astype(jnp.float32) * to_end.transpose(1, 2, 0)[:, :, :, None]).astype(
        jnp.bfloat16
    )
    fresh = jnp.einsum("cjhp,cjn->chpn", weighted, key_blocks, preferred_element_type=jnp.float32)
    starts = []
    attained_limit = []
    running = jnp.zeros((local_heads, HEAD_DIM, STATE), jnp.float32)
    product = jnp.ones((local_heads,), jnp.float32)
    for block in range(blocks):
        starts.append(running)
        attained_limit.append(product)
        running = through[:, block, None, None] * running + fresh[block]
        product = product * through[:, block]
    local_starts = jnp.stack(starts)
    reach = jnp.stack(attained_limit, axis=0)
    query_float = query_blocks.astype(jnp.float32)
    start_weight = from_start.transpose(1, 2, 0)[:, :, :, None]
    decays = lax.all_gather(product[None], "seq", axis=0, tiled=True)
    shard_count = decays.shape[0]
    rank = lax.axis_index("seq")
    shard_ids = jnp.arange(shard_count)
    between = (shard_ids[None, :] > shard_ids[:, None]) & (shard_ids[None, :] < rank)
    factors = jnp.where(between[:, :, None], decays[None, :, :], 1.0)
    weights = jnp.prod(factors, axis=1) * (shard_ids < rank).astype(jnp.float32)[:, None]
    empty = jnp.zeros((local_heads, HEAD_DIM, STATE), jnp.float32)
    incoming = empty + jnp.einsum(
        "jh,jhpn->hpn",
        weights,
        lax.all_gather(running[None].astype(jnp.bfloat16), "seq", axis=0, tiled=True).astype(
            jnp.float32
        ),
        precision=lax.Precision.HIGHEST,
    )
    full_starts = local_starts + reach[:, :, None, None] * incoming[None]
    inter = (
        jnp.einsum("cin,chpn->cihp", query_float, full_starts, precision=lax.Precision.HIGHEST)
        * start_weight
    )
    result = intra + inter + skip[None, None, :, None] * raw_values.astype(jnp.float32)
    ssm_out = result.reshape(tokens_here, local_heads * HEAD_DIM)
    gated = ssm_out * jax.nn.silu(gate_branch.astype(jnp.float32))
    squared_values = lax.psum(jnp.sum(gated * gated, axis=1), "head")
    hidden = (
        gated * lax.rsqrt(squared_values[:, None] / INNER + 1e-05) * norm_gain[None, :]
    ).astype(jnp.bfloat16)
    return lax.psum_scatter(
        jnp.dot(hidden, out_weight, preferred_element_type=jnp.float32).astype(jnp.bfloat16),
        "head",
        scatter_dimension=0,
        tiled=True,
    )


def solution(mesh):
    in_specs = (
        P("seq", "head"),
        P("seq", "head"),
        P("seq", None),
        P("seq", None),
        P("head", "seq"),
        P("seq"),
        P("head"),
        P("head"),
        P("head"),
        P("head", None),
    )
    out_specs = P(("seq", "head"), None)
    return jax.shard_map(local, mesh=mesh, in_specs=in_specs, out_specs=out_specs, check_vma=False)
```

profile of v0, /device:TPU:0, one launch (start us, length us, event | category | flops | bytes accessed | tf_op | source)
XLA Modules:
  0.0 202.5 jit_solution(18144942277648591626)
XLA Ops:
  7.2 0.9 multiply_minimum_fusion
  8.2 2.3 %reduce-window.16 = f32[16,4,2,128]{3,0,1,2:T(8,128)S(1)} reduce-window(f32[16,4,2,128]{3,0,1,2:T(8,128)S(1)} %copy.61, f32[]{:T(128)} %constant.12.clone.1), window={size=1x1x1x128 pad=0_0x0_0x0_0x127_0}, to_apply=%region_2.3 | reduce-window | flops 2080768 | bytes 131076 | tf_op jit(solution)/shard_map/reduce-window.2
  11.0 2.3 %reduce-window.14 = s32[4,2,128]{2,1,0:T(2,128)S(1)} reduce-window(s32[4,2,128]{2,1,0:T(2,128)} %bitcast.105, s32[]{:T(128)} %constant.11.clone.1), window={size=1x1x128 pad=0_0x0_0x127_0}, to_apply=%region_0.0 | reduce-window | flops 130048 | bytes 8196 | tf_op jit(solution)/shard_map/reduce-window
  14.1 4.1 %copy.58 = f32[1024,1024]{0,1:T(8,128)} copy(bf16[1024,1024]{1,0:T(8,128)(2,1)} %param.10) | data formatting | bytes 6291456 | tf_op jit(solution)/shard_map/convert_element_type | solution.py:34
  18.2 5.6 %reshape.272 = f32[4,256,16,64]{1,0,3,2:T(4,128)} reshape(f32[1024,1024]{0,1:T(8,128)} %copy.58) | data formatting | bytes 8388608 | tf_op jit(solution)/shard_map/convert_element_type | solution.py:34
  24.5 4.9 %multiply_convert_fusion.3 = (bf16[4,256,16,64]{1,0,3,2:T(4,128)(2,1)S(1)}, bf16[4,256,16,64]{1,0,3,2:T(4,128)(2,1)}) fusion(f32[4,256,16]{1,0,2:T(4,128)S(1)} %copy.65, f32[4,256,16,64]{1,0,3,2:T(4,128)} %reshape.272, f32[4,256,16]{1,0,2:T(4,128)S(1)} %bitcast.100), kind=kLoop, calls=%fused_computation.20 | loop fusion | flops 5242880 | bytes 8519680 | tf_op jit(solution)/shard_map/convert_element_type | solution.py:42
  29.4 0.7 fusion.20
  30.1 1.0 fusion.29
  31.8 22.3 %all-gather = f32[8,1,16]{2,1,0:T(1,128)S(1)} all-gather(f32[1,1,16]{2,1,0:T(1,128)S(1)} %get-tuple-element.9), channel_id=1, replica_groups=mesh['seq'=8,'head'=4] {'seq'}, dimensions={0}, use_global_device_ids=true | all-gather | bytes 576 | tf_op jit(solution)/shard_map/all_gather | solution.py:59
  55.4 3.0 %copy.69 = bf16[1024,1024]{0,1:T(8,128)(2,1)S(1)} copy(bf16[1024,1024]{1,0:T(8,128)(2,1)} %param.11) | data formatting | bytes 4194304 | tf_op args[1]
  58.4 0.7 pad_maximum_fusion
  59.2 1.0 compare_and_fusion
  60.2 2.3 %fusion.37 = f32[4,256,256]{2,1,0:T(8,128)} fusion(bf16[4,256,128]{2,1,0:T(8,128)(2,1)S(1)} %bitcast.93, bf16[4,256,128]{2,1,0:T(8,128)(2,1)} %bitcast.98), kind=kOutput, calls=%fused_computation.82 | convolution fusion | flops 67108864 | bytes 1572864 | tf_op jit(solution)/shard_map/cin,cjn->cij/dot_general | solution.py:29
  62.4 21.0 %all-gather.3.cloned.1.call-done = bf16[8,16,64,128]{3,2,1,0:T(8,128)(2,1)} async-done(((bf16[1,16,64,128]{3,2,1,0:T(8,128)(2,1)}), bf16[8,16,64,128]{3,2,1,0:T(8,128)(2,1)}) %all-gather.3.cloned.1.call-update) | async-done | bytes 2097168 | tf_op jit(solution)/shard_map/all_gather | solution.py:70
  83.4 4.2 %fusion.18 = f32[16,1,64,128]{3,1,2,0:T(1,128)S(1)} fusion(f32[8,16,1,1]{0,2,3,1:T(1,128)S(1)} %copy.71, bf16[8,16,64,128]{3,2,1,0:T(8,128)(2,1)} %all-gather.3.cloned.1.call-done), kind=kOutput, calls=%fused_computation.29 | convolution fusion | flops 12582912 | bytes 2621952 | tf_op jit(solution)/shard_map/jh,jhpn->hpn/dot_general | solution.py:67
  87.7 3.0 %fusion.12 = f32[4,16,64,256]{3,2,1,0:T(8,128)S(1)} fusion(bf16[4,256,128,1]{2,1,3,0:T(8,128)(2,1)S(1)} %bitcast.92, f32[1,16,64,128]{3,2,1,0:T(8,128)S(1)} %get-tuple-element.6, f32[1,16,64,128]{3,2,1,0:T(8,128)S(1)} %get-tuple-element.7, f32[1,16,64,128]{3,2,1,0:T(8,128)} %get-tuple-element.8, f32[4]{0:T(128)S(1)} %copy-done.7, ...), kind=kOutput, calls=%fused_computation.23 | convolution fusion | flops 1613234176 | bytes 6553872 | tf_op jit(solution)/shard_map/cin,chpn->cihp/dot_general | solution.py:77
  90.7 5.6 %fusion.11 = f32[4,256,16,64]{1,3,2,0:T(8,128)S(1)} fusion(f32[4,16,64,256]{3,2,1,0:T(8,128)S(1)} %fusion.12, f32[4,256,16,64]{1,0,3,2:T(4,128)S(1)} %copy-done.1, f32[4,256,256]{2,1,0:T(8,128)S(1)} %copy-done.4, f32[16,4,256]{2,0,1:T(8,128)S(1)} %copy_bitcast_fusion, pred[4,256,256]{2,1,0:T(8,128)(4,1)S(1)} %copy-done.6, ...), kind=kOutput, calls=%fused_computation.16 | convolution fusion | flops 562036736 | bytes 16121920 | tf_op jit(solution)/shard_map/hcij,cjhp->cihp/dot_general | solution.py:36
  96.4 3.0 %copy.68 = f32[4,256,16,64]{1,0,3,2:T(4,128)S(1)} copy(f32[4,256,16,64]{1,3,2,0:T(8,128)S(1)} %fusion.11) | data formatting | bytes 8388608 | tf_op jit(solution)/shard_map/add | solution.py:80
  99.4 1.0 copy.78
  100.4 2.0 copy-done.2
  102.4 1.3 multiply_reduce_fusion
  103.7 5.7 %psum.7 = f32[1024]{0:T(1024)S(1)} all-reduce(f32[1024]{0:T(1024)S(1)} %multiply_reduce_fusion), channel_id=1, replica_groups=mesh['seq'=8,'head'=4] {'head'}, use_global_device_ids=true, to_apply=%region_6.7 | all-reduce | flops 1024 | bytes 8192 | tf_op jit(solution)/shard_map/psum | solution.py:83
  109.4 15.9 %convolution_convert_fusion = bf16[1024,4096]{1,0:T(8,128)(2,1)} fusion(bf16[1024,4096]{1,0:T(8,128)(2,1)} %param.19, f32[1024]{0:T(1024)S(1)} %copy-done.8, f32[1024]{0:T(1024)S(1)} %add_rsqrt_fusion, f32[1024,1024]{0,1:T(8,128)} %bitcast.95, bf16[1024,1024]{0,1:T(8,128)(2,1)S(1)} %copy.69), kind=kOutput, calls=%fused_computation.7 | convolution fusion | flops 8603566080 | bytes 23076864 | tf_op jit(solution)/shard_map/dot_general | solution.py:88
  125.3 70.3 %reduce-scatter.2.cloned.1.call-done = bf16[256,4096]{1,0:T(8,128)(2,1)} async-done(((bf16[1024,4096]{1,0:T(8,128)(2,1)}), bf16[256,4096]{1,0:T(8,128)(2,1)}) %reduce-scatter.2.cloned.1.call-update) | async-done | bytes 2097168 | tf_op jit(solution)/shard_map/reduce_scatter | solution.py:87
  (57 shorter events, 4.6 us)
Async XLA Ops:
  6.5 53.6 %copy-start = (bf16[1024,128]{1,0:T(8,128)(2,1)S(1)}, bf16[1024,128]{1,0:T(8,128)(2,1)}, u32[]{:S(2)}) copy-start(bf16[1024,128]{1,0:T(8,128)(2,1)} %param.13) | copy-start | bytes 786436
  6.5 76.8 %all-gather.3.cloned.1.call-start = ((), (), s32[]{:S(2)}) async-start(), calls=%async_computation.1 | async-start | bytes 2359296 | tf_op jit(solution)/shard_map/all_gather | solution.py:70
  24.5 4.9 %copy-start.5 = (bf16[1024,128]{1,0:T(8,128)(2,1)S(1)}, bf16[1024,128]{1,0:T(8,128)(2,1)}, u32[]{:S(2)}) copy-start(bf16[1024,128]{1,0:T(8,128)(2,1)} %param.12) | copy-start | bytes 786436
  31.2 164.5 %reduce-scatter.2.cloned.1.call-start = ((), (), s32[]{:S(2)}) async-start(), calls=%async_computation.2 | async-start | bytes 10485760 | tf_op jit(solution)/shard_map/reduce_scatter | solution.py:87
  60.2 27.5 %copy-start.7 = (f32[4]{0:T(128)S(1)}, f32[4]{0:T(128)}, u32[]{:S(2)}) copy-start(f32[4]{0:T(128)} %pad.4.clone) | copy-start | bytes 52
  83.4 7.3 %copy-start.1 = (f32[4,256,16,64]{1,0,3,2:T(4,128)S(1)}, f32[4,256,16,64]{1,0,3,2:T(4,128)}, u32[]{:S(2)}) copy-start(f32[4,256,16,64]{1,0,3,2:T(4,128)} %reshape.272) | copy-start | bytes 12582916
  83.4 7.3 %copy-start.3 = (bf16[4,256,16,64]{1,0,3,2:T(4,128)(2,1)S(1)}, bf16[4,256,16,64]{1,0,3,2:T(4,128)(2,1)}, u32[]{:S(2)}) copy-start(bf16[4,256,16,64]{1,0,3,2:T(4,128)(2,1)} %get-tuple-element.13) | copy-start | bytes 6291460
  83.4 7.3 %copy-start.4 = (f32[4,256,256]{2,1,0:T(8,128)S(1)}, f32[4,256,256]{2,1,0:T(8,128)}, u32[]{:S(2)}) copy-start(f32[4,256,256]{2,1,0:T(8,128)} %fusion.37) | copy-start | bytes 3145732
  83.4 7.3 %copy-start.6 = (pred[4,256,256]{2,1,0:T(8,128)(4,1)S(1)}, pred[4,256,256]{2,1,0:T(8,128)(4,1)}, u32[]{:S(2)}) copy-start(pred[4,256,256]{2,1,0:T(8,128)(4,1)} %compare_and_fusion) | copy-start | bytes 786436
  83.4 7.3 %copy-start.9 = (f32[16]{0:T(128)S(1)}, f32[16]{0:T(128)}, u32[]{:S(2)}) copy-start(f32[16]{0:T(128)} %param.17) | copy-start | bytes 196
  100.4 2.0 copy-start.2
  100.4 9.0 %copy-start.8 = (f32[1024]{0:T(1024)S(1)}, f32[1024]{0:T(1024)}, u32[]{:S(2)}) copy-start(f32[1024]{0:T(1024)} %param.18) | copy-start | bytes 12292
Sparse Core Ops, SparseCore 0:
  31.3 52.0 all-gather.2
  125.4 70.1 reduce-scatter.1
where the time goes:
time: 203 us; the launch traced here: 202 us
  waiting for transfers between devices  91.4 us (45%)
  matrix products  31.7 us (16%)
  blocking collectives  27.9 us (14%)
  local copies, waits for them, and re-layouts  20.8 us (10%)
  other arithmetic  17 us (8%)
  between operations  13.6 us (7%)
    reduce_scatter x1, waiting for transfers between devices, local(): lax.psum_scatter(jnp.dot(hidden, out_weight, preferred_element_type=jnp.f...  70.3 us
    all_gather x1, blocking collectives, local(): decays = lax.all_gather(product[None], 'seq', axis=0, tiled=True)  22.3 us
    all_gather x1, waiting for transfers between devices, local(): lax.all_gather(running[None].astype(jnp.bfloat16), 'seq', axis=0, tiled=T...  21 us
    dot_general x1, matrix products, local(): jnp.dot(hidden, out_weight, preferred_element_type=jnp.float32)  15.9 us
    convert_element_type x2, local copies, waits for them, and re-layouts, local(): scaled = (raw_values.astype(jnp.float32) * step_scale).astype(jnp.bfloat16)  9.75 us
    unnamed x24, local copies, waits for them, and re-layouts  6.13 us
    psum x1, blocking collectives, local(): squared_values = lax.psum(jnp.sum(gated * gated, axis=1), 'head')  5.67 us
    dot_general x1, matrix products, local(): jnp.einsum('hcij,cjhp->cihp', scores, scaled, preferred_element_type=jnp....  5.64 us
  transfers between devices with their start and end apart: 2, of which 2 were waited for; matrix products, arithmetic and copies ran while one was open for 4% of the time, Pallas kernels for 0%

commit v1 on v0

v1 whole, which is shorter than its diff:
```python
import functools

import jax
import jax.numpy as jnp
from jax import lax
from jax.experimental import pallas as pl
from jax.experimental.pallas import tpu as pltpu
from jax.sharding import PartitionSpec as P

HEAD_DIM = 64
SPAN = 256
QUARTERS = 4
F32 = jnp.float32
BF16 = jnp.bfloat16
MESH = pl.DeviceIdType.MESH
VMEM_BYTES = 60 * 1024 * 1024


def dot_nt(a, b):
    return lax.dot_general(a, b, (((1,), (1,)), ((), ())), preferred_element_type=F32)


def dot_tn(a, b):
    return lax.dot_general(a, b, (((0,), (0,)), ((), ())), preferred_element_type=F32)


def dot_nn(a, b):
    return jnp.dot(a, b, preferred_element_type=F32)


def two_pieces(v):
    high = v.astype(BF16)
    low = (v - high.astype(F32)).astype(BF16)
    return jnp.concatenate([high, low], axis=1)


def spread(heads):
    rows = lax.broadcasted_iota(jnp.int32, (2 * heads, heads * HEAD_DIM), 0)
    columns = lax.broadcasted_iota(jnp.int32, (2 * heads, heads * HEAD_DIM), 1)
    own = (columns // HEAD_DIM == rows) | (columns // HEAD_DIM == rows - heads)
    return jnp.where(own, 1.0, 0.0).astype(BF16)


def digits(code, flags):
    low = code & 127
    middle = (code >> 7) & 127
    high = code >> 14
    extra = jnp.broadcast_to(flags, code.shape)
    rows = jnp.concatenate([low, middle, high, extra], axis=0)
    return rows.astype(F32).astype(BF16)


def joined(sums, heads, axis):
    def take(n):
        return lax.slice_in_dim(sums, n * heads, (n + 1) * heads, axis=axis)

    return (take(0) + 128.0 * take(1) + 16384.0 * take(2)), take(3)


def final_kernel(x_ref, b_ref, code_ref, code_col_ref, flag_ref, rate_row_ref, rate_col_ref, out_ref):
    heads, ticks = code_ref.shape
    code = code_ref[...]
    parts = digits(code, flag_ref[...])
    i = lax.broadcasted_iota(jnp.int32, (ticks, ticks), 0)
    j = lax.broadcasted_iota(jnp.int32, (ticks, ticks), 1)
    later = jnp.where(j > i, 1.0, 0.0).astype(BF16)
    after, seen = joined(dot_nt(later, parts), heads, 1)
    scale = jnp.minimum(code_col_ref[...].astype(F32) / 16.0, 1.0)
    factor = jnp.where(seen == 0.0, jnp.exp(-rate_row_ref[...] * (after / 16.0)), 0.0) * scale
    wide = dot_nn(two_pieces(factor), spread(heads))
    weighted = (x_ref[...].astype(F32) * wide).astype(BF16)
    state = dot_tn(weighted, b_ref[...])
    rows = state.shape[0]
    out_ref[0:rows, :] = state.astype(BF16)
    every = jnp.ones((state.shape[1], ticks), BF16)
    total, resets = joined(dot_nt(parts, every), heads, 0)
    through = jnp.where(resets == 0.0, jnp.exp(-rate_col_ref[...] * (total / 16.0)), 0.0)
    high = through.astype(BF16)
    rest = through - high.astype(F32)
    middle = rest.astype(BF16)
    low = (rest - middle.astype(F32)).astype(BF16)
    lane = lax.broadcasted_iota(jnp.int32, through.shape, 1)
    packed = jnp.where(lane == 0, high.astype(F32), jnp.where(lane == 1, middle.astype(F32), low.astype(F32)))
    out_ref[rows : rows + heads, :] = packed.astype(BF16)


def intra_kernel(
    x_ref, b_ref, c_ref, code_ref, code_col_ref, flag_ref, rate_row_ref, rate_col_ref, skip_ref,
    ssm_ref, reach_ref, state, gone,
):
    heads = code_ref.shape[0]

    @pl.when(pl.program_id(0) == 0)
    def _():
        state[...] = jnp.zeros_like(state)
        gone[...] = jnp.zeros_like(gone)

    parts = digits(code_ref[...], flag_ref[...])
    i = lax.broadcasted_iota(jnp.int32, (SPAN, SPAN), 0)
    j = lax.broadcasted_iota(jnp.int32, (SPAN, SPAN), 1)
    upto = jnp.where(j <= i, 1.0, 0.0).astype(BF16)
    later = jnp.where(j > i, 1.0, 0.0).astype(BF16)
    sum_col, count_col = joined(dot_nt(upto, parts), heads, 1)
    after_col, seen_after = joined(dot_nt(later, parts), heads, 1)
    sum_row, count_row = joined(dot_nt(parts, upto), heads, 0)
    rate_row = rate_row_ref[...]
    cum_col = -rate_row * (sum_col / 16.0)
    cum_row = -rate_col_ref[...] * (sum_row / 16.0)
    eye = spread(heads)
    scale = jnp.minimum(code_col_ref[...].astype(F32) / 16.0, 1.0)
    to_end = jnp.where(seen_after == 0.0, jnp.exp(-rate_row * (after_col / 16.0)), 0.0)
    from_start = jnp.where(count_col == 0.0, jnp.exp(cum_col), 0.0)
    last = jnp.where(
        count_col[SPAN - 1 : SPAN] == 0.0, jnp.exp(cum_col[SPAN - 1 : SPAN]), 0.0
    )

    x = x_ref[...].astype(F32)
    wide_scale = dot_nn(scale.astype(BF16), eye[0:heads])
    scaled = (x * wide_scale).astype(BF16)
    b = b_ref[...]
    c = c_ref[...]
    linked = (count_col[:, 0:1] == count_row[0:1, :]) & (j <= i)
    cross = jnp.where(linked, dot_nt(c, b), 0.0)
    left = lax.broadcasted_iota(jnp.int32, (SPAN, 2 * HEAD_DIM), 1) < HEAD_DIM
    for pair in range(heads // 2):
        columns = slice(pair * 2 * HEAD_DIM, (pair + 1) * 2 * HEAD_DIM)
        both = scaled[:, columns]
        sides = []
        for h in (2 * pair, 2 * pair + 1):
            gap = jnp.minimum(cum_col[:, h : h + 1] - cum_row[h : h + 1, :], 0.0)
            scores = (jnp.exp(gap) * cross).astype(BF16)
            sides.append(dot_nn(scores, both))
        ssm_ref[:, columns] = jnp.where(left, sides[0], sides[1])
    old = state[...]
    carried = dot_nt(c, old.astype(BF16)) * dot_nn(two_pieces(from_start), eye)
    ssm_ref[...] = ssm_ref[...] + carried + skip_ref[...] * x
    weighted = (scaled.astype(F32) * dot_nn(two_pieces(to_end), eye)).astype(BF16)
    fresh = dot_tn(weighted, b)
    keep = dot_tn(eye, jnp.transpose(two_pieces(jnp.broadcast_to(last, (128, heads))).astype(F32)).astype(BF16))
    state[...] = keep * old + fresh
    before = gone[0:1, :]
    broken = gone[1:2, :]
    whole = jnp.where(
        (count_col + broken) == 0.0, jnp.exp(-rate_row * ((sum_col + before) / 16.0)), 0.0
    )
    reach_ref[...] = two_pieces(whole)
    gone[0:1, :] = before + sum_col[SPAN - 1 : SPAN]
    gone[1:2, :] = broken + count_col[SPAN - 1 : SPAN]


def mix_kernel(
    shards, seq_of, ssm_ref, gate_ref, c_ref, reach_ref, all_ref, gain_ref, w_hbm, out_ref,
    w, mine, incoming, kept, send1, recv1, send2, recv2, sq_send, sq_recv,
    w_sem, s1, r1, s2, r2, sqs, sqr,
):
    me = lax.axis_index("head")
    rank = lax.axis_index("seq")
    core = me % 2
    half = me // 2
    partner = half * 2 + (1 - core)
    across = (1 - half) * 2 + core
    diagonal = (1 - half) * 2 + (1 - core)
    inner = gate_ref.shape[1]
    width = out_ref.shape[1] // QUARTERS
    heads = inner // HEAD_DIM

    def load(q):
        return pltpu.make_async_copy(w_hbm.at[:, pl.ds(q * width, width)], w.at[q], w_sem.at[q])

    for q in range(QUARTERS):
        load(q).start()
    barrier = pltpu.get_barrier_semaphore()
    for other in (partner, across, diagonal):
        pl.semaphore_signal(barrier, inc=1, device_id={"head": other}, device_id_type=MESH)
    pl.semaphore_wait(barrier, 3)

    eye = spread(heads)
    incoming[...] = jnp.zeros_like(incoming)

    def take(n, _):
        pieces = all_ref[n, pl.ds(inner, heads), :].astype(F32)
        decay = pieces[:, 0:1] + pieces[:, 1:2] + pieces[:, 2:3]
        early = (n < rank).astype(F32)
        decay = early * decay + (1.0 - early)
        for h in range(heads):
            rows = slice(h * HEAD_DIM, (h + 1) * HEAD_DIM)
            fresh = all_ref[n, rows, :].astype(F32)
            incoming[rows, :] = decay[h : h + 1, :] * incoming[rows, :] + early * fresh
        return 0

    lax.fori_loop(0, shards, take, 0)
    start = incoming[...].astype(BF16)

    def prepare(block, slot):
        rows = pl.ds(pl.multiple_of(block * SPAN, SPAN), SPAN)
        carried = dot_nt(c_ref[rows, :], start) * dot_nn(reach_ref[rows, :], eye)
        gate = gate_ref[rows, :].astype(F32)
        gated = (ssm_ref[rows, :] + carried) * (gate / (1.0 + jnp.exp(-gate)))
        mine[...] = (gated * gain_ref[...]).astype(BF16)
        square = gated * gated
        high = square.astype(BF16)
        low = (square - high.astype(F32)).astype(BF16)
        ones = jnp.ones((8, inner), BF16)
        sq_send[slot] = dot_nt(ones, high) + dot_nt(ones, low)

    def square_copy(slot, other):
        return pltpu.make_async_remote_copy(
            src_ref=sq_send.at[slot], dst_ref=sq_recv.at[slot], send_sem=sqs.at[slot],
            recv_sem=sqr.at[slot], device_id={"head": other}, device_id_type=MESH,
        )

    def to_partner(turn, q):
        return pltpu.make_async_remote_copy(
            src_ref=send1.at[turn, q], dst_ref=recv1.at[turn, q], send_sem=s1.at[turn, q],
            recv_sem=r1.at[turn, q], device_id={"head": partner}, device_id_type=MESH,
        )

    def to_across(q):
        return pltpu.make_async_remote_copy(
            src_ref=send2.at[q], dst_ref=recv2.at[q], send_sem=s2.at[q],
            recv_sem=r2.at[q], device_id={"head": across}, device_id_type=MESH,
        )

    prepare(diagonal, 0)
    square_copy(0, diagonal).start()
    for q in range(QUARTERS):
        load(q).wait()

    def first(q, _):
        send1[0, q] = dot_nn(mine[...], w[q]).astype(BF16)
        to_partner(0, q).start()
        return 0

    lax.fori_loop(0, QUARTERS, first, 0)
    prepare(across, 1)
    square_copy(1, across).start()

    def second(q, _):
        part = dot_nn(mine[...], w[q])
        to_partner(0, q).wait_recv()
        send2[q] = (part + recv1[0, q].astype(F32)).astype(BF16)
        to_across(q).start()
        return 0

    lax.fori_loop(0, QUARTERS, second, 0)
    prepare(partner, 2)
    square_copy(2, partner).start()

    def third(q, _):
        send1[1, q] = dot_nn(mine[...], w[q]).astype(BF16)
        to_partner(1, q).start()
        return 0

    lax.fori_loop(0, QUARTERS, third, 0)
    prepare(me, 3)

    def fourth(q, _):
        part = dot_nn(mine[...], w[q])
        to_partner(1, q).wait_recv()
        kept[q] = part + recv1[1, q].astype(F32)
        return 0

    lax.fori_loop(0, QUARTERS, fourth, 0)
    for slot, other in enumerate((diagonal, across, partner)):
        square_copy(slot, other).wait()
    total = (sq_send[3] + sq_recv[0] + sq_recv[1] + sq_recv[2])[0:1, :]
    norm = lax.rsqrt(total / (4 * inner) + 1e-05)
    i = lax.broadcasted_iota(jnp.int32, (SPAN, SPAN), 0)
    j = lax.broadcasted_iota(jnp.int32, (SPAN, SPAN), 1)
    column = jnp.sum(jnp.where(i == j, norm, 0.0), axis=1, keepdims=True)
    for q in range(QUARTERS):
        to_across(q).wait_recv()
        out_ref[:, q * width : (q + 1) * width] = (
            (kept[q] + recv2[q].astype(F32)) * column
        ).astype(BF16)
    for q in range(QUARTERS):
        to_partner(0, q).wait_send()
        to_partner(1, q).wait_send()
        to_across(q).wait_send()


def local(shards, xs, gate_branch, bmat, cmat, dt_code, resets, decay_rate, skip, norm_gain, out_weight):
    ticks, inner = xs.shape
    heads = dt_code.shape[0]
    size = bmat.shape[1]
    model = out_weight.shape[1]
    code_col = dt_code.T
    flags = resets[None, :]
    rate_row = decay_rate[None, :]
    rate_col = decay_rate[:, None]
    wide_skip = jnp.repeat(skip, HEAD_DIM)[None, :]
    vmem = pl.BlockSpec(memory_space=pltpu.VMEM)
    final = pl.pallas_call(
        final_kernel,
        out_shape=jax.ShapeDtypeStruct((inner + heads, size), BF16),
        in_specs=[vmem] * 7,
        out_specs=vmem,
        compiler_params=pltpu.CompilerParams(vmem_limit_bytes=VMEM_BYTES),
        name="final_state",
    )(xs, bmat, dt_code, code_col, flags, rate_row, rate_col)
    gathered = lax.all_gather(final, "seq", axis=0, tiled=False)

    def whole(shape):
        return pl.BlockSpec(shape, lambda b: (0, 0))

    ssm, reach = pl.pallas_call(
        intra_kernel,
        grid=(ticks // SPAN,),
        out_shape=(
            jax.ShapeDtypeStruct((ticks, inner), F32),
            jax.ShapeDtypeStruct((ticks, 2 * heads), BF16),
        ),
        in_specs=[
            pl.BlockSpec((SPAN, inner), lambda b: (b, 0)),
            pl.BlockSpec((SPAN, size), lambda b: (b, 0)),
            pl.BlockSpec((SPAN, size), lambda b: (b, 0)),
            pl.BlockSpec((heads, SPAN), lambda b: (0, b)),
            pl.BlockSpec((SPAN, heads), lambda b: (b, 0)),
            pl.BlockSpec((1, SPAN), lambda b: (0, b)),
            whole((1, heads)),
            whole((heads, 1)),
            whole((1, inner)),
        ],
        out_specs=(
            pl.BlockSpec((SPAN, inner), lambda b: (b, 0)),
            pl.BlockSpec((SPAN, 2 * heads), lambda b: (b, 0)),
        ),
        scratch_shapes=[pltpu.VMEM((inner, size), F32), pltpu.VMEM((8, heads), F32)],
        compiler_params=pltpu.CompilerParams(vmem_limit_bytes=VMEM_BYTES // 2),
        cost_estimate=pl.CostEstimate(
            flops=12_000_000_000, bytes_accessed=8_000_000, transcendentals=5_000_000
        ),
        name="intra",
    )(xs, bmat, cmat, dt_code, code_col, flags, rate_row, rate_col, wide_skip)
    width = model // QUARTERS
    dma = pltpu.SemaphoreType.DMA
    return pl.pallas_call(
        functools.partial(mix_kernel, shards, None),
        out_shape=jax.ShapeDtypeStruct((SPAN, model), BF16),
        in_specs=[vmem] * 6 + [pl.BlockSpec(memory_space=pl.ANY)],
        out_specs=vmem,
        scratch_shapes=[
            pltpu.VMEM((QUARTERS, inner, width), BF16),
            pltpu.VMEM((SPAN, inner), BF16),
            pltpu.VMEM((inner, size), F32),
            pltpu.VMEM((QUARTERS, SPAN, width), F32),
            pltpu.VMEM((2, QUARTERS, SPAN, width), BF16),
            pltpu.VMEM((2, QUARTERS, SPAN, width), BF16),
            pltpu.VMEM((QUARTERS, SPAN, width), BF16),
            pltpu.VMEM((QUARTERS, SPAN, width), BF16),
            pltpu.VMEM((4, 8, SPAN), F32),
            pltpu.VMEM((3, 8, SPAN), F32),
            dma((QUARTERS,)),
            dma((2, QUARTERS)),
            dma((2, QUARTERS)),
            dma((QUARTERS,)),
            dma((QUARTERS,)),
            dma((3,)),
            dma((3,)),
        ],
        compiler_params=pltpu.CompilerParams(
            collective_id=0, has_side_effects=True, vmem_limit_bytes=VMEM_BYTES
        ),
        name="mix",
    )(ssm, gate_branch, cmat, reach, gathered, norm_gain[None, :], out_weight)


def solution(mesh):
    in_specs = (
        P("seq", "head"),
        P("seq", "head"),
        P("seq", None),
        P("seq", None),
        P("head", "seq"),
        P("seq"),
        P("head"),
        P("head"),
        P("head"),
        P("head", None),
    )
    out_specs = P(("seq", "head"), None)
    return jax.shard_map(
        functools.partial(local, mesh.shape["seq"]),
        mesh=mesh, in_specs=in_specs, out_specs=out_specs, check_vma=False,
    )
```

time: 203 us -> 139 us (0.68)
  Pallas kernels: 0 us -> 76.3 us
  waiting for transfers between devices: 91.4 us -> 40 us
  matrix products: 31.7 us -> 0 us
  blocking collectives: 27.9 us -> 0 us
  other arithmetic: 17 us -> 0 us
  local copies, waits for them, and re-layouts: 20.8 us -> 9.28 us
    pallas_call x0 -> x3, Pallas kernels: none -> 76.3 us  [the longest x1 60.9 us: local(): pl.pallas_call(functools.partial(mix_kernel, shards, None), out_shape=jax...]
    reduce_scatter x1 -> x0, waiting for transfers between devices: 70.3 us -> none  [local(): lax.psum_scatter(jnp.dot(hidden, out_weight, preferred_element_type=jnp.f...]
    dot_general x6 -> x0, matrix products: 31.7 us -> none  [the longest x1 15.9 us: local(): jnp.dot(hidden, out_weight, preferred_element_type=jnp.float32)]
    all_gather x1 -> x0, blocking collectives: 22.3 us -> none  [local(): decays = lax.all_gather(product[None], 'seq', axis=0, tiled=True)]
    all_gather x1, waiting for transfers between devices: 21 us -> 40 us  [local(): gathered = lax.all_gather(final, 'seq', axis=0, tiled=False)]
    convert_element_type x2 -> x0, local copies, waits for them, and re-layouts: 9.75 us -> none  [local(): scaled = (raw_values.astype(jnp.float32) * step_scale).astype(jnp.bfloat16)]
    another operation x7 -> x0, other arithmetic: 6 us -> none
    convert_element_type x2 -> x0, other arithmetic: 5.97 us -> none  [the longest x1 4.92 us: local(): (scaled.astype(jnp.float32) * to_end.transpose(1, 2, 0)[:, :, :, None]).a...]
  transfers between devices with their start and end apart: 2 -> 1, of which waited for: 2 -> 1; matrix products, arithmetic and copies ran while one was open for 4% -> 0% of each run, Pallas kernels for 0% -> 7%
where the time goes in v1:
time: 139 us
  Pallas kernels  76.3 us (55%)
  waiting for transfers between devices  40 us (29%)
  between operations  13.5 us (10%)
  local copies, waits for them, and re-layouts  9.28 us (7%)
    pallas_call x1, Pallas kernels, local(): pl.pallas_call(functools.partial(mix_kernel, shards, None), out_shape=jax...  60.9 us
    all_gather x1, waiting for transfers between devices, local(): gathered = lax.all_gather(final, 'seq', axis=0, tiled=False)  40 us
    pallas_call x1, Pallas kernels, local(): pl.pallas_call(intra_kernel, grid=(ticks // SPAN,), out_shape=(jax.ShapeD...  9.45 us
    unnamed x24, local copies, waits for them, and re-layouts  7.66 us
    pallas_call x1, Pallas kernels, local(): pl.pallas_call(final_kernel, out_shape=jax.ShapeDtypeStruct((inner + head...  5.9 us
  transfers between devices with their start and end apart: 1, of which 1 were waited for; matrix products, arithmetic and copies ran while one was open for 0% of the time, Pallas kernels for 7%

profile of v1, /device:TPU:0, one launch (start us, length us, event | category | flops | bytes accessed | tf_op | source)
XLA Modules:
  0.0 139.1 jit_solution(9331121819391503179)
XLA Ops:
  6.6 0.0 copy-start.10
  6.6 0.0 copy-start.3
  6.6 0.0 all-gather.3.cloned.1.call-start
  6.6 1.5 %copy.12.rate_col_ref = f32[16,1]{1,0:T(8,128)} copy(f32[16,1]{0,1:T(1,128)} %bitcast.10) | data formatting | bytes 128 | tf_op jit(solution)/shard_map/broadcast_in_dim | solution.py:290
  8.1 1.9 %copy.11 = s32[16,1024]{0,1:T(8,128)} copy(s32[16,1024]{1,0:T(8,128)} %code_ref.3) | data formatting | bytes 131072 | tf_op args[4]
  9.9 5.9 %final_state.1 = bf16[1040,128]{1,0:T(8,128)(2,1)} custom-call(bf16[1024,1024]{1,0:T(8,128)(2,1)} %x_ref.3, bf16[1024,128]{1,0:T(8,128)(2,1)} %b_ref.3, s32[16,1024]{1,0:T(8,128)} %code_ref.3, s32[1024,16]{1,0:T(8,128)} %bitcast.6, s32[1,1024]{1,0:T(1,128)} %bitcast.8, f32[1,16]{1,0:T(1,128)} %bitcast.11, f32[16,1]{1,0:T(8,128)} %copy.12.rate_col_ref), custom_call_target="tpu_custom_call" | custom-call | tf_op jit(solution)/shard_map/final_state/pallas_call | solution.py:293
  15.8 0.0 all-gather.3.cloned.1.call-update
  15.9 0.0 copy-done.10
  15.9 0.1 broadcast_in_dim.18
  16.0 0.1 broadcast_in_dim_reshape.3.skip_ref
  16.0 0.0 copy-done.9
  16.0 0.0 copy-done.5
  16.0 0.0 copy-done.6
  16.0 0.0 copy-done.1
  16.1 0.0 copy-done.8
  16.1 0.0 copy-done.3
  16.1 0.0 copy-done.7
  16.1 0.0 copy-done.2
  16.1 9.4 %intra.1 = (f32[1024,1024]{1,0:T(8,128)S(1)}, bf16[1024,32]{1,0:T(8,128)(2,1)S(1)}) custom-call(bf16[1024,1024]{1,0:T(8,128)(2,1)S(1)} %copy-done.1, bf16[1024,128]{1,0:T(8,128)(2,1)S(1)} %copy-done.6, bf16[1024,128]{1,0:T(8,128)(2,1)S(1)} %copy-done.3, s32[16,1024]{1,0:T(8,128)S(1)} %copy-done.5, s32[1024,16]{1,0:T(8,128)S(1)} %bitcast.7, ...), custom_call_target="tpu_custom_call" | custom-call | flops 12000000000 | bytes 8000000 | tf_op jit(solution)/shard_map/intra/pallas_call | solution.py:306
  25.6 1.9 %copy-done = f32[1024,1024]{1,0:T(8,128)} copy-done((f32[1024,1024]{1,0:T(8,128)}, f32[1024,1024]{1,0:T(8,128)S(1)}, u32[]{:S(2)}) %copy-start) | copy-done | bytes 4194328
  27.5 0.7 copy-done.4
  28.2 40.0 %all-gather.3.cloned.1.call-done = bf16[8320,128]{1,0:T(8,128)(2,1)} async-done(((bf16[1040,128]{1,0:T(8,128)(2,1)}), bf16[8320,128]{1,0:T(8,128)(2,1)}) %all-gather.3.cloned.1.call-update) | async-done | bytes 2129936 | tf_op jit(solution)/shard_map/all_gather | solution.py:301
  68.2 60.9 %mix.1 = bf16[256,4096]{1,0:T(8,128)(2,1)} custom-call(f32[1024,1024]{1,0:T(8,128)} %copy-done, bf16[1024,1024]{1,0:T(8,128)(2,1)} %gate_ref.1, bf16[1024,128]{1,0:T(8,128)(2,1)} %c_ref.3, bf16[1024,32]{1,0:T(8,128)(2,1)} %copy-done.4, bf16[8,1040,128]{2,1,0:T(8,128)(2,1)} %bitcast.13, f32[1,1024]{1,0:T(1,128)} %bitcast.14, bf16[1024,4096]{1,0:T(8,128)(2,1)} %w_hbm.1), custom_call_target="tpu_custom_call" | custom-call | tf_op jit(solution)/shard_map/mix/pallas_call | solution.py:337
  129.1 3.1 %copy.15 = bf16[256,4096]{1,0:T(8,128)(2,1)} copy(bf16[256,4096]{1,0:T(8,128)(2,1)} %mix.1) | data formatting | bytes 4194304
  (9 shorter events, 0.0 us)
Async XLA Ops:
  6.5 9.5 %copy-start.9 = (f32[16]{0:T(128)S(1)}, f32[16]{0:T(128)}, u32[]{:S(2)}) copy-start(f32[16]{0:T(128)} %param.16) | copy-start | bytes 196
  6.5 9.5 %copy-start.5 = (s32[16,1024]{1,0:T(8,128)S(1)}, s32[16,1024]{1,0:T(8,128)}, u32[]{:S(2)}) copy-start(s32[16,1024]{1,0:T(8,128)} %code_ref.3) | copy-start | bytes 196612
  6.5 9.5 %copy-start.6 = (bf16[1024,128]{1,0:T(8,128)(2,1)S(1)}, bf16[1024,128]{1,0:T(8,128)(2,1)}, u32[]{:S(2)}) copy-start(bf16[1024,128]{1,0:T(8,128)(2,1)} %b_ref.3) | copy-start | bytes 786436
  6.5 9.5 %copy-start.1 = (bf16[1024,1024]{1,0:T(8,128)(2,1)S(1)}, bf16[1024,1024]{1,0:T(8,128)(2,1)}, u32[]{:S(2)}) copy-start(bf16[1024,1024]{1,0:T(8,128)(2,1)} %x_ref.3) | copy-start | bytes 6291460
  6.5 9.5 %copy-start.8 = (s32[1024]{0:T(1024)S(1)}, s32[1024]{0:T(1024)}, u32[]{:S(2)}) copy-start(s32[1024]{0:T(1024)} %param.15) | copy-start | bytes 12292
  6.6 9.3 %copy-start.10 = (f32[16]{0:T(128)S(1)}, f32[16]{0:T(128)}, u32[]{:S(2)}) copy-start(f32[16]{0:T(128)} %param.17) | copy-start | bytes 196
  6.6 9.5 %copy-start.3 = (bf16[1024,128]{1,0:T(8,128)(2,1)S(1)}, bf16[1024,128]{1,0:T(8,128)(2,1)}, u32[]{:S(2)}) copy-start(bf16[1024,128]{1,0:T(8,128)(2,1)} %c_ref.3) | copy-start | bytes 786436
  6.6 61.6 %all-gather.3.cloned.1.call-start = ((), (), s32[]{:S(2)}) async-start(), calls=%async_computation | async-start | bytes 2396160 | tf_op jit(solution)/shard_map/all_gather | solution.py:301
  8.1 8.0 %copy-start.7 = (f32[16,1]{1,0:T(8,128)S(1)}, f32[16,1]{1,0:T(8,128)}, u32[]{:S(2)}) copy-start(f32[16,1]{1,0:T(8,128)} %copy.12.rate_col_ref) | copy-start | bytes 196
  9.9 6.1 %copy-start.2 = (s32[16,1024]{0,1:T(8,128)S(1)}, s32[16,1024]{0,1:T(8,128)}, u32[]{:S(2)}) copy-start(s32[16,1024]{0,1:T(8,128)} %copy.11) | copy-start | bytes 196612
  25.6 1.9 %copy-start = (f32[1024,1024]{1,0:T(8,128)}, f32[1024,1024]{1,0:T(8,128)S(1)}, u32[]{:S(2)}) copy-start(f32[1024,1024]{1,0:T(8,128)S(1)} %get-tuple-element.7.ssm_ref) | copy-start | bytes 12582916
  27.5 0.7 copy-start.4
Sparse Core Ops, SparseCore 0:
  16.0 52.1 all-gather.2

commit v2 on v1

v2 whole, which is shorter than its diff:
```python
import functools

import jax
import jax.numpy as jnp
from jax import lax
from jax.experimental import pallas as pl
from jax.experimental.pallas import tpu as pltpu
from jax.sharding import PartitionSpec as P

HEAD_DIM = 64
SPAN = 256
QUARTERS = 4
F32 = jnp.float32
BF16 = jnp.bfloat16
MESH = pl.DeviceIdType.MESH
VMEM_BYTES = 60 * 1024 * 1024


def dot_nt(a, b):
    return lax.dot_general(a, b, (((1,), (1,)), ((), ())), preferred_element_type=F32)


def dot_tn(a, b):
    return lax.dot_general(a, b, (((0,), (0,)), ((), ())), preferred_element_type=F32)


def dot_nn(a, b):
    return jnp.dot(a, b, preferred_element_type=F32)


def two_pieces(v):
    high = v.astype(BF16)
    low = (v - high.astype(F32)).astype(BF16)
    return jnp.concatenate([high, low], axis=1)


def spread(heads):
    rows = lax.broadcasted_iota(jnp.int32, (2 * heads, heads * HEAD_DIM), 0)
    columns = lax.broadcasted_iota(jnp.int32, (2 * heads, heads * HEAD_DIM), 1)
    own = (columns // HEAD_DIM == rows) | (columns // HEAD_DIM == rows - heads)
    return jnp.where(own, 1.0, 0.0).astype(BF16)


def digits(code, flags):
    low = code & 127
    middle = (code >> 7) & 127
    high = code >> 14
    extra = jnp.broadcast_to(flags, code.shape)
    rows = jnp.concatenate([low, middle, high, extra], axis=0)
    return rows.astype(F32).astype(BF16)


def joined(sums, heads, axis):
    def take(n):
        return lax.slice_in_dim(sums, n * heads, (n + 1) * heads, axis=axis)

    return (take(0) + 128.0 * take(1) + 16384.0 * take(2)), take(3)


def layer_kernel(
    shards, x_ref, gate_ref, b_ref, c_ref, code_ref, flag_ref, rate_ref, skip_ref, gain_ref, w_hbm, out_ref,
    w, ssm, reach, own, state, gone, final, other_final, decay, other_decay, came, passed, incoming,
    mine, kept, send1, recv1, send2, recv2, sq_send, sq_recv,
    w_sem, fs, fr, ds, dr, cs, cr, s1, r1, s2, r2, sqs, sqr,
):
    me = lax.axis_index("head")
    rank = lax.axis_index("seq")
    core = me % 2
    half = me // 2
    partner = half * 2 + (1 - core)
    across = (1 - half) * 2 + core
    diagonal = (1 - half) * 2 + (1 - core)
    odd = rank % 2
    twin = rank + 1 - 2 * odd
    ticks, inner = x_ref.shape
    heads = code_ref.shape[0]
    width = out_ref.shape[1] // QUARTERS
    blocks = ticks // SPAN
    pieces = heads // 2
    piece = inner // pieces

    def load(q):
        return pltpu.make_async_copy(w_hbm.at[:, pl.ds(q * width, width)], w.at[q], w_sem.at[q])

    for q in range(QUARTERS):
        load(q).start()

    @pl.when(rank < 2)
    def _():
        came[...] = jnp.zeros_like(came)

    barrier = pltpu.get_barrier_semaphore()
    for other in (partner, across, diagonal):
        pl.semaphore_signal(barrier, inc=1, device_id={"head": other}, device_id_type=MESH)
    for other in (twin, (rank + 2) % shards, (rank + shards - 2) % shards):
        pl.semaphore_signal(barrier, inc=1, device_id={"seq": other}, device_id_type=MESH)

    eye = spread(heads)
    rate_row = rate_ref[...]
    hi = lax.broadcasted_iota(jnp.int32, (heads, heads), 0)
    hj = lax.broadcasted_iota(jnp.int32, (heads, heads), 1)
    rate_col = jnp.sum(jnp.where(hi == hj, rate_row, 0.0), axis=1, keepdims=True)
    wide_skip = dot_nn(two_pieces(jnp.broadcast_to(skip_ref[...], (8, heads))), eye)[0:1]

    def scales(codes):
        return jnp.transpose(jnp.minimum(codes.astype(F32) / 16.0, 1.0))

    def local_final():
        parts = digits(code_ref[...], flag_ref[...])
        i = lax.broadcasted_iota(jnp.int32, (ticks, ticks), 0)
        j = lax.broadcasted_iota(jnp.int32, (ticks, ticks), 1)
        later = jnp.where(j > i, 1.0, 0.0).astype(BF16)
        after, seen = joined(dot_nt(later, parts), heads, 1)
        factor = jnp.where(seen == 0.0, jnp.exp(-rate_row * (after / 16.0)), 0.0)
        factor = factor * scales(code_ref[...])
        wide = dot_nn(two_pieces(factor), eye)
        weighted = (x_ref[...].astype(F32) * wide).astype(BF16)
        whole = dot_tn(weighted, b_ref[...])
        own[...] = whole
        final[...] = whole.astype(BF16)
        every = jnp.ones((whole.shape[1], ticks), BF16)
        total, resets = joined(dot_nt(parts, every), heads, 0)
        decay[...] = jnp.where(resets == 0.0, jnp.exp(-rate_col * (total / 16.0)), 0.0)

    def final_copy(q):
        rows = pl.ds(q * piece, piece)
        return pltpu.make_async_remote_copy(
            src_ref=final.at[rows], dst_ref=other_final.at[rows], send_sem=fs.at[q],
            recv_sem=fr.at[q], device_id={"seq": twin}, device_id_type=MESH,
        )

    def decay_copy():
        return pltpu.make_async_remote_copy(
            src_ref=decay, dst_ref=other_decay, send_sem=ds.at[0],
            recv_sem=dr.at[0], device_id={"seq": twin}, device_id_type=MESH,
        )

    def chain_copy(q):
        rows = pl.ds(q * piece, piece)
        return pltpu.make_async_remote_copy(
            src_ref=passed.at[rows], dst_ref=came.at[rows], send_sem=cs.at[q],
            recv_sem=cr.at[q], device_id={"seq": (rank + 2) % shards}, device_id_type=MESH,
        )

    local_final()
    pl.semaphore_wait(barrier, 6)
    decay_copy().start()
    for q in range(pieces):
        final_copy(q).start()

    state[...] = jnp.zeros_like(state)
    gone[...] = jnp.zeros_like(gone)

    def intra(block, _):
        start = pl.multiple_of(block * SPAN, SPAN)
        rows = pl.ds(start, SPAN)
        codes = code_ref[:, rows]
        parts = digits(codes, flag_ref[:, rows])
        i = lax.broadcasted_iota(jnp.int32, (SPAN, SPAN), 0)
        j = lax.broadcasted_iota(jnp.int32, (SPAN, SPAN), 1)
        upto = jnp.where(j <= i, 1.0, 0.0).astype(BF16)
        later = jnp.where(j > i, 1.0, 0.0).astype(BF16)
        sum_col, count_col = joined(dot_nt(upto, parts), heads, 1)
        after_col, seen_after = joined(dot_nt(later, parts), heads, 1)
        sum_row, count_row = joined(dot_nt(parts, upto), heads, 0)
        cum_col = -rate_row * (sum_col / 16.0)
        cum_row = -rate_col * (sum_row / 16.0)
        to_end = jnp.where(seen_after == 0.0, jnp.exp(-rate_row * (after_col / 16.0)), 0.0)
        from_start = jnp.where(count_col == 0.0, jnp.exp(cum_col), 0.0)
        last = jnp.where(
            count_col[SPAN - 1 : SPAN] == 0.0, jnp.exp(cum_col[SPAN - 1 : SPAN]), 0.0
        )
        x = x_ref[rows, :].astype(F32)
        scaled = (x * dot_nn(scales(codes).astype(BF16), eye[0:heads])).astype(BF16)
        b = b_ref[rows, :]
        c = c_ref[rows, :]
        linked = (count_col[:, 0:1] == count_row[0:1, :]) & (j <= i)
        cross = jnp.where(linked, dot_nt(c, b), 0.0)
        left = lax.broadcasted_iota(jnp.int32, (SPAN, 2 * HEAD_DIM), 1) < HEAD_DIM
        old = state[...]
        carried = dot_nt(c, old.astype(BF16)) * dot_nn(two_pieces(from_start), eye)
        carried = carried + wide_skip * x
        for pair in range(heads // 2):
            columns = slice(pair * 2 * HEAD_DIM, (pair + 1) * 2 * HEAD_DIM)
            both = scaled[:, columns]
            sides = []
            for h in (2 * pair, 2 * pair + 1):
                gap = jnp.minimum(cum_col[:, h : h + 1] - cum_row[h : h + 1, :], 0.0)
                scores = (jnp.exp(gap) * cross).astype(BF16)
                sides.append(dot_nn(scores, both))
            ssm[rows, columns] = jnp.where(left, sides[0], sides[1]) + carried[:, columns]
        weighted = (scaled.astype(F32) * dot_nn(two_pieces(to_end), eye)).astype(BF16)
        fresh = dot_tn(weighted, b)
        spread_last = two_pieces(jnp.broadcast_to(last, (128, heads))).astype(F32)
        state[...] = dot_tn(eye, jnp.transpose(spread_last).astype(BF16)) * old + fresh
        before = gone[0:1, :]
        broken = gone[1:2, :]
        whole = jnp.where(
            (count_col + broken) == 0.0, jnp.exp(-rate_row * ((sum_col + before) / 16.0)), 0.0
        )
        reach[rows, :] = two_pieces(whole)
        gone[0:1, :] = before + sum_col[SPAN - 1 : SPAN]
        gone[1:2, :] = broken + count_col[SPAN - 1 : SPAN]
        return 0

    lax.fori_loop(0, blocks - 1, intra, 0)

    decay_copy().wait_recv()
    odd_f = odd.astype(F32)
    even_f = 1.0 - odd_f
    ours = decay[...]
    theirs = other_decay[...]
    second_decay = odd_f * ours + even_f * theirs
    both_decay = ours * theirs
    step_decay = odd_f * theirs + even_f
    for q in range(pieces):
        final_copy(q).wait_recv()

        @pl.when(rank >= 2)
        def _():
            chain_copy(q).wait_recv()

        for h in range(2 * q, 2 * q + 2):
            rows = slice(h * HEAD_DIM, (h + 1) * HEAD_DIM)
            here = own[rows, :]
            there = other_final[rows, :].astype(F32)
            before = came[rows, :].astype(F32)
            first = odd_f * there + even_f * here
            second = odd_f * here + even_f * there
            total = second_decay[h : h + 1, :] * first + second
            passed[rows, :] = (both_decay[h : h + 1, :] * before + total).astype(BF16)
            incoming[rows, :] = (step_decay[h : h + 1, :] * before + odd_f * there).astype(BF16)

        @pl.when(rank < shards - 2)
        def _():
            chain_copy(q).start()

    lax.fori_loop(blocks - 1, blocks, intra, 0)
    start = incoming[...]

    def prepare(block, slot):
        rows = pl.ds(pl.multiple_of(block * SPAN, SPAN), SPAN)
        carried = dot_nt(c_ref[rows, :], start) * dot_nn(reach[rows, :], eye)
        gate = gate_ref[rows, :].astype(F32)
        gated = (ssm[rows, :] + carried) * (gate / (1.0 + jnp.exp(-gate)))
        mine[...] = (gated * gain_ref[...]).astype(BF16)
        square = gated * gated
        high = square.astype(BF16)
        low = (square - high.astype(F32)).astype(BF16)
        ones = jnp.ones((8, inner), BF16)
        sq_send[slot] = dot_nt(ones, high) + dot_nt(ones, low)

    def square_copy(slot, other):
        return pltpu.make_async_remote_copy(
            src_ref=sq_send.at[slot], dst_ref=sq_recv.at[slot], send_sem=sqs.at[slot],
            recv_sem=sqr.at[slot], device_id={"head": other}, device_id_type=MESH,
        )

    def to_partner(turn, q):
        return pltpu.make_async_remote_copy(
            src_ref=send1.at[turn, q], dst_ref=recv1.at[turn, q], send_sem=s1.at[turn, q],
            recv_sem=r1.at[turn, q], device_id={"head": partner}, device_id_type=MESH,
        )

    def to_across(q):
        return pltpu.make_async_remote_copy(
            src_ref=send2.at[q], dst_ref=recv2.at[q], send_sem=s2.at[q],
            recv_sem=r2.at[q], device_id={"head": across}, device_id_type=MESH,
        )

    prepare(diagonal, 0)
    square_copy(0, diagonal).start()
    for q in range(QUARTERS):
        load(q).wait()

    def first(q, _):
        send1[0, q] = dot_nn(mine[...], w[q]).astype(BF16)
        to_partner(0, q).start()
        return 0

    lax.fori_loop(0, QUARTERS, first, 0)
    prepare(across, 1)
    square_copy(1, across).start()

    def second(q, _):
        part = dot_nn(mine[...], w[q])
        to_partner(0, q).wait_recv()
        send2[q] = (part + recv1[0, q].astype(F32)).astype(BF16)
        to_across(q).start()
        return 0

    lax.fori_loop(0, QUARTERS, second, 0)
    prepare(partner, 2)
    square_copy(2, partner).start()

    def third(q, _):
        send1[1, q] = dot_nn(mine[...], w[q]).astype(BF16)
        to_partner(1, q).start()
        return 0

    lax.fori_loop(0, QUARTERS, third, 0)
    prepare(me, 3)

    def fourth(q, _):
        part = dot_nn(mine[...], w[q])
        to_partner(1, q).wait_recv()
        kept[q] = part + recv1[1, q].astype(F32)
        return 0

    lax.fori_loop(0, QUARTERS, fourth, 0)
    for slot, other in enumerate((diagonal, across, partner)):
        square_copy(slot, other).wait()
    total = (sq_send[3] + sq_recv[0] + sq_recv[1] + sq_recv[2])[0:1, :]
    norm = lax.rsqrt(total / (4 * inner) + 1e-05)
    i = lax.broadcasted_iota(jnp.int32, (SPAN, SPAN), 0)
    j = lax.broadcasted_iota(jnp.int32, (SPAN, SPAN), 1)
    column = jnp.sum(jnp.where(i == j, norm, 0.0), axis=1, keepdims=True)
    for q in range(QUARTERS):
        to_across(q).wait_recv()
        out_ref[:, q * width : (q + 1) * width] = (
            (kept[q] + recv2[q].astype(F32)) * column
        ).astype(BF16)
    for q in range(QUARTERS):
        to_partner(0, q).wait_send()
        to_partner(1, q).wait_send()
        to_across(q).wait_send()
    for q in range(pieces):
        final_copy(q).wait_send()
    decay_copy().wait_send()

    @pl.when(rank < shards - 2)
    def _():
        for q in range(pieces):
            chain_copy(q).wait_send()


def local(shards, xs, gate_branch, bmat, cmat, dt_code, resets, decay_rate, skip, norm_gain, out_weight):
    ticks, inner = xs.shape
    heads = dt_code.shape[0]
    size = bmat.shape[1]
    model = out_weight.shape[1]
    width = model // QUARTERS
    pieces = heads // 2
    vmem = pl.BlockSpec(memory_space=pltpu.VMEM)
    dma = pltpu.SemaphoreType.DMA
    return pl.pallas_call(
        functools.partial(layer_kernel, shards),
        out_shape=jax.ShapeDtypeStruct((SPAN, model), BF16),
        in_specs=[vmem] * 9 + [pl.BlockSpec(memory_space=pl.ANY)],
        out_specs=vmem,
        scratch_shapes=[
            pltpu.VMEM((QUARTERS, inner, width), BF16),
            pltpu.VMEM((ticks, inner), F32),
            pltpu.VMEM((ticks, 2 * heads), BF16),
            pltpu.VMEM((inner, size), F32),
            pltpu.VMEM((inner, size), F32),
            pltpu.VMEM((8, heads), F32),
            pltpu.VMEM((inner, size), BF16),
            pltpu.VMEM((inner, size), BF16),
            pltpu.VMEM((heads, size), F32),
            pltpu.VMEM((heads, size), F32),
            pltpu.VMEM((inner, size), BF16),
            pltpu.VMEM((inner, size), BF16),
            pltpu.VMEM((inner, size), BF16),
            pltpu.VMEM((SPAN, inner), BF16),
            pltpu.VMEM((QUARTERS, SPAN, width), F32),
            pltpu.VMEM((2, QUARTERS, SPAN, width), BF16),
            pltpu.VMEM((2, QUARTERS, SPAN, width), BF16),
            pltpu.VMEM((QUARTERS, SPAN, width), BF16),
            pltpu.VMEM((QUARTERS, SPAN, width), BF16),
            pltpu.VMEM((4, 8, SPAN), F32),
            pltpu.VMEM((3, 8, SPAN), F32),
            dma((QUARTERS,)),
            dma((pieces,)),
            dma((pieces,)),
            dma((1,)),
            dma((1,)),
            dma((pieces,)),
            dma((pieces,)),
            dma((2, QUARTERS)),
            dma((2, QUARTERS)),
            dma((QUARTERS,)),
            dma((QUARTERS,)),
            dma((3,)),
            dma((3,)),
        ],
        compiler_params=pltpu.CompilerParams(
            collective_id=0, has_side_effects=True, vmem_limit_bytes=VMEM_BYTES
        ),
        name="layer",
    )(
        xs, gate_branch, bmat, cmat, dt_code, resets[None, :], decay_rate[None, :], skip[None, :],
        norm_gain[None, :], out_weight,
    )


def solution(mesh):
    in_specs = (
        P("seq", "head"),
        P("seq", "head"),
        P("seq", None),
        P("seq", None),
        P("head", "seq"),
        P("seq"),
        P("head"),
        P("head"),
        P("head"),
        P("head", None),
    )
    out_specs = P(("seq", "head"), None)
    return jax.shard_map(
        functools.partial(local, mesh.shape["seq"]),
        mesh=mesh, in_specs=in_specs, out_specs=out_specs, check_vma=False,
    )
```

time: 139 us -> 84.8 us (0.61)
  the two profiles are of different devices: /device:TPU:0 before, /device:TPU:26 now
where the time goes in v2:
time: 84.8 us; the launch traced here: 84.6 us
  Pallas kernels  81.5 us (96%)
  local copies, waits for them, and re-layouts  3.13 us (4%)
    pallas_call x1, Pallas kernels, local(): pl.pallas_call(functools.partial(layer_kernel, shards), out_shape=jax.Sha...  81.5 us
    unnamed x1, local copies, waits for them, and re-layouts  3.13 us

profile of v2, /device:TPU:26, one launch (start us, length us, event | category | flops | bytes accessed | tf_op | source)
XLA Modules:
  0.0 84.6 jit_solution(7948976412170406140)
XLA Ops:
  0.0 81.5 %layer.1 = bf16[256,4096]{1,0:T(8,128)(2,1)} custom-call(bf16[1024,1024]{1,0:T(8,128)(2,1)} %x_ref.1, bf16[1024,1024]{1,0:T(8,128)(2,1)} %gate_ref.1, bf16[1024,128]{1,0:T(8,128)(2,1)} %b_ref.1, bf16[1024,128]{1,0:T(8,128)(2,1)} %c_ref.1, s32[16,1024]{1,0:T(8,128)} %code_ref.1, s32[1,1024]{1,0:T(1,128)} %bitcast.4, f32[1,16]{1,0:T(1,128)} %bitcast.6, ...), custom_call_target="tpu_custom_call" | custom-call | tf_op jit(solution)/shard_map/layer/pallas_call | solution.py:346
  81.5 3.1 %copy.12 = bf16[256,4096]{1,0:T(8,128)(2,1)} copy(bf16[256,4096]{1,0:T(8,128)(2,1)} %layer.1) | data formatting | bytes 4194304
